TPU v7x, 32 devices: a whole 2x2x4 slice. The times are simulated.
32 devices in a mesh: dp: 8 (over z, x), mp: 4 (over y, core).
Axes of the slice: x: 2, y: 2, z: 4, core: 2. Of those that a mesh axis runs over, the one named last changes fastest.
Arguments:
- sparse_vecs: bfloat16 [8192, 26, 128], P(('dp', 'mp')), may hold values from -6 to 6
- dense_vec: bfloat16 [8192, 128], P(('dp', 'mp')), may hold values from -6 to 6
- top_cot: bfloat16 [8192, 1024], P(('dp', 'mp')), may hold values from -0.59765625 to 0.59765625
- top_weight: bfloat16 [479, 1024], replicated, may hold values from -0.25 to 0.25
- owner_ids: int32 [8192, 26, 1], P(('dp', 'mp')), may hold values from 0 to 7; in each aligned block of 6656 rows (0 to 6655, 6656 to 13311, ..., all dimensions but the last counted through in order) at most 1664 rows name the same one
- local_rows: int32 [8192, 26], P(('dp', 'mp')), may hold values from 0 to 127
- table: float32 [26, 1024, 128], P(None, ('dp', 'mp')), may hold values from -0.6 to 0.6
- accum: float32 [26, 1024], P(None, ('dp', 'mp')), may hold values from 0.05 to 2
Outputs:
- dense_grad: bfloat16 [8192, 128], P(('dp', 'mp'))
- new_table: float32 [26, 1024, 128], P(None, ('dp', 'mp'))
- new_accum: float32 [26, 1024], P(None, ('dp', 'mp'))
Inputs may be any that keep to these rules, and one draw needn't show every extreme that they name: `owner_ids`: among the lookups of one device's 256 samples no owner group is named more than 1664 times; in every draw some device names some owner group exactly 1664 times.
All inputs are finite; a program needn't handle non-finite values.
Results may differ from a plain program's by a relative error of at most 0.005.
Values may be sent and summed in bfloat16 or wider, within the bound.
A program may use at most 128 MiB of HBM per device.

v0:
```python
import jax
import jax.numpy as jnp
import numpy as np
from jax import lax
from jax.sharding import PartitionSpec as P

LEARN_RATE = 0.1
EPSILON = 1e-08


def pair_matrix(feature_count):
    row_index, col_index = np.tril_indices(feature_count, -1)
    pair_count = row_index.shape[0]
    matrix = np.zeros((pair_count, feature_count * feature_count), np.float32)
    matrix[np.arange(pair_count), row_index * feature_count + col_index] = 1.0
    matrix[np.arange(pair_count), col_index * feature_count + row_index] = 1.0
    return jnp.asarray(matrix)


def accumulate(grad_rows, grad_keys, first_col, columns):
    sources, capacity, row_width = grad_rows.shape
    most_rows = max(1, 4096 // capacity)
    per_turn = 1
    while per_turn * 2 <= most_rows and sources % (per_turn * 2) == 0:
        per_turn = per_turn * 2
    turn_count = sources // per_turn
    row_blocks = grad_rows.reshape(turn_count, per_turn * capacity, row_width)
    key_blocks = grad_keys.reshape(turn_count, per_turn * capacity) - first_col
    targets = jnp.arange(columns, dtype=jnp.int32)[None, :]

    def add_block(turn_index, running):
        row_piece = lax.dynamic_index_in_dim(row_blocks, turn_index, 0, keepdims=False)
        key_piece = lax.dynamic_index_in_dim(key_blocks, turn_index, 0, keepdims=False)
        onehot = (key_piece[:, None] == targets).astype(jnp.bfloat16)
        return running + lax.dot_general(
            onehot, row_piece, (((0,), (0,)), ((), ())), preferred_element_type=jnp.float32
        )

    return lax.fori_loop(0, turn_count, add_block, jnp.zeros((columns, row_width), jnp.float32))


def slot_ranks(target, dp_count):
    lookups = target.shape[0]
    block_len = min(512, lookups)
    block_count = (lookups + block_len - 1) // block_len
    padded_len = block_count * block_len
    padded_target = jnp.concatenate([target, jnp.full((padded_len - lookups,), -1, jnp.int32)])
    member = (padded_target[:, None] == jnp.arange(dp_count, dtype=jnp.int32)[None, :]).astype(
        jnp.bfloat16
    )
    member_blocks = member.reshape(block_count, block_len, dp_count)
    lower = (jnp.arange(block_len)[:, None] >= jnp.arange(block_len)[None, :]).astype(jnp.bfloat16)
    within = jnp.einsum("ij,bjd->bid", lower, member_blocks, preferred_element_type=jnp.float32)
    block_totals = within[:, block_len - 1, :]
    strict = (jnp.arange(block_count)[:, None] > jnp.arange(block_count)[None, :]).astype(
        jnp.float32
    )
    offsets = jnp.dot(
        strict, block_totals, precision=lax.Precision.HIGHEST, preferred_element_type=jnp.float32
    )
    counts = (within + offsets[:, None, :]) * member_blocks.astype(jnp.float32)
    ranks = jnp.sum(counts, axis=2).reshape(padded_len)
    return ranks.astype(jnp.int32) - 1


def per_device(sparse_vecs, dense_vec, top_cot, top_weight, owner_ids, local_rows, table, accum):
    batch_rows, table_count, row_width = sparse_vecs.shape
    feature_count = table_count + 1
    input_cot = jnp.einsum("bh,zh->bz", top_cot, top_weight, preferred_element_type=jnp.float32)
    symmetric = jnp.dot(
        input_cot[:, row_width:],
        pair_matrix(feature_count),
        precision=lax.Precision.HIGHEST,
        preferred_element_type=jnp.float32,
    )
    symmetric = symmetric.reshape(batch_rows, feature_count, feature_count)
    features = jnp.concatenate([dense_vec[:, None, :], sparse_vecs], axis=1).astype(jnp.float32)
    feature_grad = jnp.einsum("bij,bje->bie", symmetric, features, precision=lax.Precision.HIGHEST)
    dense_grad = (input_cot[:, :row_width] + feature_grad[:, 0]).astype(jnp.bfloat16)
    sparse_grad = feature_grad[:, 1:].astype(jnp.bfloat16)
    dp_count = lax.axis_size("dp")
    rows_own = table.shape[1]
    own_cols = table_count * rows_own
    lookups = batch_rows * table_count
    capacity = 2 * lookups // dp_count
    slot_total = dp_count * capacity
    target = owner_ids.reshape(lookups)
    table_pos = jnp.arange(table_count, dtype=jnp.int32)[None, :]
    column = (
        local_rows // rows_own * own_cols + table_pos * rows_own + local_rows % rows_own
    ).reshape(lookups)
    slot_index = target * capacity + slot_ranks(target, dp_count)
    source_of = (
        jnp.full((slot_total,), -1, jnp.int32)
        .at[slot_index]
        .set(jnp.arange(lookups, dtype=jnp.int32))
    )
    filled = source_of >= 0
    safe_source = jnp.maximum(source_of, 0)
    send_rows = jnp.take(sparse_grad.reshape(lookups, row_width), safe_source, axis=0)
    send_rows = jnp.where(filled[:, None], send_rows, jnp.zeros_like(send_rows))
    send_keys = jnp.where(filled, jnp.take(column, safe_source, axis=0), -1)
    send_rows = send_rows.reshape(dp_count, capacity, row_width)
    send_keys = send_keys.reshape(dp_count, capacity)
    recv_rows, recv_keys = (
        lax.all_to_all(send_rows, "dp", split_axis=0, concat_axis=0, tiled=True),
        lax.all_to_all(send_keys, "dp", split_axis=0, concat_axis=0, tiled=True),
    )
    row_grad = lax.psum_scatter(
        accumulate(recv_rows, recv_keys, jnp.int32(0), lax.axis_size("mp") * own_cols).astype(
            jnp.bfloat16
        ),
        "mp",
        scatter_dimension=0,
        tiled=True,
    ).astype(jnp.float32)
    row_grad = row_grad.reshape(table_count, rows_own, row_width)
    new_accum = accum + jnp.mean(row_grad * row_grad, axis=-1)
    new_table = table - LEARN_RATE * row_grad / (jnp.sqrt(new_accum)[:, :, None] + EPSILON)
    return (dense_grad, new_table, new_accum)


def solution(mesh):
    in_specs = (
        P(("dp", "mp"), None, None),
        P(("dp", "mp"), None),
        P(("dp", "mp"), None),
        P(),
        P(("dp", "mp"), None, None),
        P(("dp", "mp"), None),
        P(None, ("dp", "mp"), None),
        P(None, ("dp", "mp")),
    )
    out_specs = (P(("dp", "mp"), None), P(None, ("dp", "mp"), None), P(None, ("dp", "mp")))
    return jax.shard_map(
        per_device, mesh=mesh, in_specs=in_specs, out_specs=out_specs, check_vma=False
    )
```

profile of v0, /device:TPU:0, one launch (start us, length us, event | category | flops | bytes accessed | tf_op | source)
XLA Modules:
  0.0 365.2 jit_solution(838342878156029762)
XLA Ops:
  7.2 0.0 copy-start
  7.2 0.8 broadcast_multiply_fusion
  8.0 0.9 copy.33
  8.9 0.8 fusion.22
  9.7 0.1 copy.36
  9.8 0.1 reshape.121
  10.0 0.1 copy.32
  10.1 0.2 mul.48
  10.3 0.1 eq.60
  10.4 0.3 convolution_bitcast_fusion
  10.7 0.1 slice.28
  10.8 0.1 copy.34
  10.9 0.1 fusion.30
  11.0 0.2 multiply_reduce_fusion
  11.3 0.1 fusion.27
  11.4 24.9 %scatter_custom_fusion = s32[13312]{0:T(1024)S(1)} fusion(s32[6656]{0:T(1024)S(1)} %fusion.27, s32[6656]{0:T(1024)S(1)} %iota.39, s32[]{:T(128)} %constant.98.clone.1), kind=kCustom, calls=%fused_computation.53 | custom fusion | bytes 53252 | tf_op jit(solution)/shard_map/scatter | solution.py:96
  36.3 0.0 copy-start.2
  36.3 73.7 %gather_fusion = s32[13312]{0:T(1024)S(1)} fusion(s32[6656]{0:T(1024)S(1)} %reshape.121, s32[13312]{0:T(1024)S(1)} %maximum_clamp_fusion), kind=kCustom, calls=%fused_computation | custom fusion | bytes 159744 | tf_op jit(solution)/shard_map/jit(_take)/gather | solution.py:102
  110.0 0.6 select_select_fusion.1
  110.6 7.3 %all-to-all-start = ((s32[8,1,1664]{2,1,0:T(1,128)}), s32[8,1,1664]{2,1,0:T(1,128)S(1)}, u32[]{:S(2)}, u32[]{:S(2)}) async-start(s32[8,1,1664]{2,1,0:T(1,128)} %bitcast.5), calls=%async_computation | async-start | bytes 106496 | tf_op jit(solution)/shard_map/all_to_all | solution.py:107
  117.9 0.0 copy-done
  117.9 0.0 copy-done.2
  117.9 0.5 fusion.33
  118.4 3.3 fusion.15
  121.6 0.1 reshape.120
  121.7 4.4 %copy.30 = f32[256,27,27]{2,1,0:T(8,128)} copy(f32[256,27,27]{0,2,1:T(8,128)S(1)} %reshape.120) | data formatting | bytes 1492992 | tf_op jit(solution)/shard_map/reshape | solution.py:76
  126.2 0.0 copy-start.4
  126.2 2.6 copy.29
  128.8 0.0 copy-done.4
  128.8 0.1 copy.28
  129.0 4.5 %fusion.8 = f32[256,27,128]{2,1,0:T(8,128)S(1)} fusion(f32[256,27,27]{2,1,0:T(8,128)} %copy.30, bf16[256,26,128]{2,1,0:T(8,128)(2,1)S(1)} %copy.29, bf16[256,1,128]{2,1,0:T(2,128)(2,1)S(1)} %copy.28), kind=kOutput, calls=%fused_computation.14 | convolution fusion | flops 290193408 | bytes 6054912 | tf_op jit(solution)/shard_map/bij,bje->bie/dot_general | solution.py:78
  133.5 0.0 copy-start.1
  133.5 1.9 copy-done.1
  135.4 1.9 slice.36
  137.2 2.6 reshape.123
  139.8 46.8 %gather_fusion.1 = bf16[13312,128]{1,0:T(8,128)(2,1)} fusion(bf16[6656,128]{1,0:T(8,128)(2,1)S(1)} %reshape.123, s32[13312]{0:T(1024)S(1)} %maximum_clamp_fusion), kind=kCustom, calls=%fused_computation.1 | custom fusion | bytes 6868992 | tf_op jit(solution)/shard_map/jit(_take)/gather | solution.py:100
  186.6 0.1 broadcast_in_dim.65
  186.6 0.1 broadcast_in_dim.63
  186.7 7.0 %select_select_fusion = bf16[8,1664,128]{2,1,0:T(8,128)(2,1)} fusion(bf16[8,1664,128]{2,1,0:T(8,128)(2,1)} %bitcast.35, pred[8,1664]{1,0:T(8,128)(4,1)S(1)} %broadcast_in_dim.65, pred[8,1664]{1,0:T(8,128)(4,1)S(1)} %broadcast_in_dim.63), kind=kLoop, calls=%fused_computation.13 | loop fusion | flops 3407872 | bytes 6842368 | tf_op jit(solution)/shard_map/jit(_where)/select_n | solution.py:101
  193.7 0.0 all-to-all-done
  193.8 6.0 %all-to-all-start.1 = ((bf16[8,1664,128]{2,1,0:T(8,128)(2,1)}), bf16[8,1664,128]{2,1,0:T(8,128)(2,1)}, u32[]{:S(2)}, u32[]{:S(2)}) async-start(bf16[8,1664,128]{2,1,0:T(8,128)(2,1)} %select_select_fusion), calls=%async_computation.1 | async-start | bytes 6815744 | tf_op jit(solution)/shard_map/all_to_all | solution.py:106
  199.8 0.0 reduce-scatter.2.cloned.1.call-start
  199.8 0.1 reduce.3
  200.0 75.7 %all-to-all-done.1 = bf16[8,1664,128]{2,1,0:T(8,128)(2,1)} async-done(((bf16[8,1664,128]{2,1,0:T(8,128)(2,1)}), bf16[8,1664,128]{2,1,0:T(8,128)(2,1)}, u32[]{:S(2)}, u32[]{:S(2)}) %all-to-all-start.1) | async-done | bytes 3407904 | tf_op jit(solution)/shard_map/all_to_all | solution.py:106
  275.6 56.1 %while.14 = (s32[]{:T(128)}, f32[3328,128]{1,0:T(8,128)S(1)}, s32[4,3328]{1,0:T(4,128)S(1)}, bf16[4,3328,128]{2,1,0:T(8,128)(2,1)}, s32[]{:T(128)}, /*index=5*/s32[]{:T(128)}) while((s32[]{:T(128)}, f32[3328,128]{1,0:T(8,128)S(1)}, s32[4,3328]{1,0:T(4,128)S(1)}, bf16[4,3328,128]{2,1,0:T(8,128)(2,1)}, s32[]{:T(128)}, ...), condition=%wide.region_3.4_spmd.clone, body=%wide.region_2.3_spmd.clone.sunk | while | flops 2847277056 | bytes 4299871 | solution.py:39
  275.7 14.0 %fusion.41 = f32[3328,128]{1,0:T(8,128)S(1)} fusion(s32[3328]{0:T(1024)S(1)} %dynamic-slice_reduce_fusion.2, f32[3328,128]{1,0:T(8,128)S(1)} %get-tuple-element.171, bf16[4,3328,128]{2,1,0:T(8,128)(2,1)} %get-tuple-element.179, s32[]{:T(128)S(6)} %copy.43, pred[]{:T(512)S(6)} %compare.6), kind=kOutput, calls=%fused_computation.7.clone.1 | convolution fusion | flops 2847277056 | bytes 4273157 | tf_op jit(solution)/shard_map/while/body/eval_jaxpr/dot_general | solution.py:35
  289.7 14.0 %fusion.41 = f32[3328,128]{1,0:T(8,128)S(1)} fusion(s32[3328]{0:T(1024)S(1)} %dynamic-slice_reduce_fusion.2, f32[3328,128]{1,0:T(8,128)S(1)} %get-tuple-element.171, bf16[4,3328,128]{2,1,0:T(8,128)(2,1)} %get-tuple-element.179, s32[]{:T(128)S(6)} %copy.43, pred[]{:T(512)S(6)} %compare.6), kind=kOutput, calls=%fused_computation.7.clone.1 | convolution fusion | flops 2847277056 | bytes 4273157 | tf_op jit(solution)/shard_map/while/body/eval_jaxpr/dot_general | solution.py:35
  303.7 14.0 %fusion.41 = f32[3328,128]{1,0:T(8,128)S(1)} fusion(s32[3328]{0:T(1024)S(1)} %dynamic-slice_reduce_fusion.2, f32[3328,128]{1,0:T(8,128)S(1)} %get-tuple-element.171, bf16[4,3328,128]{2,1,0:T(8,128)(2,1)} %get-tuple-element.179, s32[]{:T(128)S(6)} %copy.43, pred[]{:T(512)S(6)} %compare.6), kind=kOutput, calls=%fused_computation.7.clone.1 | convolution fusion | flops 2847277056 | bytes 4273157 | tf_op jit(solution)/shard_map/while/body/eval_jaxpr/dot_general | solution.py:35
  317.8 14.0 %fusion.41 = f32[3328,128]{1,0:T(8,128)S(1)} fusion(s32[3328]{0:T(1024)S(1)} %dynamic-slice_reduce_fusion.2, f32[3328,128]{1,0:T(8,128)S(1)} %get-tuple-element.171, bf16[4,3328,128]{2,1,0:T(8,128)(2,1)} %get-tuple-element.179, s32[]{:T(128)S(6)} %copy.43, pred[]{:T(512)S(6)} %compare.6), kind=kOutput, calls=%fused_computation.7.clone.1 | convolution fusion | flops 2847277056 | bytes 4273157 | tf_op jit(solution)/shard_map/while/body/eval_jaxpr/dot_general | solution.py:35
  331.7 0.0 copy-start.5
  331.7 1.0 convert_element_type.38
  332.7 0.0 copy-start.3
  332.7 0.0 reduce-scatter.2.cloned.1.call-update
  332.8 1.3 slice.27
  334.1 0.1 copy.39
  334.2 0.7 copy.37
  335.0 20.7 %reduce-scatter.2.cloned.1.call-done = bf16[832,128]{1,0:T(8,128)(2,1)} async-done(((bf16[3328,128]{1,0:T(8,128)(2,1)}), bf16[832,128]{1,0:T(8,128)(2,1)}) %reduce-scatter.2.cloned.1.call-update) | async-done | bytes 213008 | tf_op jit(solution)/shard_map/reduce_scatter | solution.py:109
  355.6 1.1 fusion.14
  356.8 0.1 div.34
  356.8 0.0 copy-done.5
  356.8 0.6 sqrt_add_fusion
  357.5 0.0 copy-done.3
  357.5 0.9 divide_subtract_fusion
  (13 shorter events, 0.3 us)
Async XLA Ops:
  7.2 110.7 %copy-start = (bf16[479,1024]{1,0:T(8,128)(2,1)S(1)}, bf16[479,1024]{1,0:T(8,128)(2,1)}, u32[]{:S(2)}) copy-start(bf16[479,1024]{1,0:T(8,128)(2,1)} %param.14) | copy-start | bytes 2942980
  36.3 81.6 %copy-start.2 = (bf16[256,1024]{1,0:T(8,128)(2,1)S(1)}, bf16[256,1024]{1,0:T(8,128)(2,1)}, u32[]{:S(2)}) copy-start(bf16[256,1024]{1,0:T(8,128)(2,1)} %param.13) | copy-start | bytes 1572868
  110.6 83.1 %all-to-all-start = ((s32[8,1,1664]{2,1,0:T(1,128)}), s32[8,1,1664]{2,1,0:T(1,128)S(1)}, u32[]{:S(2)}, u32[]{:S(2)}) async-start(s32[8,1,1664]{2,1,0:T(1,128)} %bitcast.5), calls=%async_computation | async-start | bytes 106496 | tf_op jit(solution)/shard_map/all_to_all | solution.py:107
  126.2 2.6 copy-start.4
  133.5 1.9 copy-start.1
  193.8 81.9 %all-to-all-start.1 = ((bf16[8,1664,128]{2,1,0:T(8,128)(2,1)}), bf16[8,1664,128]{2,1,0:T(8,128)(2,1)}, u32[]{:S(2)}, u32[]{:S(2)}) async-start(bf16[8,1664,128]{2,1,0:T(8,128)(2,1)} %select_select_fusion), calls=%async_computation.1 | async-start | bytes 6815744 | tf_op jit(solution)/shard_map/all_to_all | solution.py:106
  199.8 155.9 %reduce-scatter.2.cloned.1.call-start = ((), (), s32[]{:S(2)}) async-start(), calls=%async_computation.3 | async-start | bytes 1064960 | tf_op jit(solution)/shard_map/reduce_scatter | solution.py:109
  331.7 25.1 %copy-start.5 = (f32[26,32]{1,0:T(8,128)S(1)}, f32[26,32]{1,0:T(8,128)}, u32[]{:S(2)}) copy-start(f32[26,32]{1,0:T(8,128)} %param.18) | copy-start | bytes 9988
  332.7 24.7 %copy-start.3 = (f32[26,32,128]{2,1,0:T(8,128)S(1)}, f32[26,32,128]{2,1,0:T(8,128)}, u32[]{:S(2)}) copy-start(f32[26,32,128]{2,1,0:T(8,128)} %param.17) | copy-start | bytes 1277956
Sparse Core Ops, SparseCore 0:
  332.9 22.6 reduce-scatter.1
where the time goes:
time: 366 us; the launch traced here: 365 us
  local copies, waits for them, and re-layouts  163 us (45%)
  waiting for transfers between devices  96.3 us (26%)
  matrix products  64.4 us (18%)
  between operations  14.3 us (4%)
  other arithmetic  13.5 us (4%)
  starting transfers between devices  13.3 us (4%)
    all_to_all x1, waiting for transfers between devices, per_device(): lax.all_to_all(send_rows, 'dp', split_axis=0, concat_axis=0, tiled=True)  75.7 us
    gather x1, local copies, waits for them, and re-layouts, per_device(): send_keys = jnp.where(filled, jnp.take(column, safe_source, axis=0), -1)  73.7 us
    dot_general x4, matrix products, add_block(): lax.dot_general(onehot, row_piece, (((0,), (0,)), ((), ())), preferred_el...  55.8 us
    gather x1, local copies, waits for them, and re-layouts, per_device(): jnp.take(sparse_grad.reshape(lookups, row_width), safe_source, axis=0)  46.8 us
    scatter x1, local copies, waits for them, and re-layouts, per_device(): source_of = jnp.full((slot_total,), -1, jnp.int32).at[slot_index].set(jnp...  24.9 us
    reduce_scatter x1, waiting for transfers between devices, per_device(): lax.psum_scatter(accumulate(recv_rows, recv_keys, jnp.int32(0), lax.axis_...  20.7 us
  transfers between devices with their start and end apart: 3, of which 2 were waited for; matrix products, arithmetic and copies ran while one was open for 21% of the time, Pallas kernels for 0%

commit v1 on v0

v1 whole, which is shorter than its diff:
```python
import functools

import jax
import jax.numpy as jnp
import numpy as np
from jax import lax
from jax.experimental import pallas as pl
from jax.experimental.pallas import tpu as pltpu
from jax.sharding import PartitionSpec as P

LEARN_RATE = 0.1
EPSILON = 1e-08
MESH = pl.DeviceIdType.MESH
CHUNKS = 2
VMEM_LIMIT = 60 * 1024 * 1024


def pair_matrix(feature_count):
    row_index, col_index = np.tril_indices(feature_count, -1)
    pair_count = row_index.shape[0]
    matrix = np.zeros((pair_count, feature_count * feature_count), np.float32)
    matrix[np.arange(pair_count), row_index * feature_count + col_index] = 1.0
    matrix[np.arange(pair_count), col_index * feature_count + row_index] = 1.0
    return jnp.asarray(matrix)


def table_chunks(table_count):
    cut = (table_count + 1) // 2
    halves = []
    for half, (low, high) in enumerate(((0, cut), (cut, table_count))):
        edges = [low + (high - low) * k // CHUNKS for k in range(CHUNKS + 1)]
        halves.append([(half, a, b - a) for a, b in zip(edges, edges[1:]) if b > a])
    out = []
    for k in range(CHUNKS):
        for pieces in halves:
            if k < len(pieces):
                out.append(pieces[k])
    return cut, out


def neighbours():
    dp, mp = lax.axis_index("dp"), lax.axis_index("mp")
    mp_count = lax.axis_size("mp")
    across_x = (dp + 1 - 2 * (dp % 2), mp)
    across_y = (dp, (mp + mp_count // 2) % mp_count)
    core = (dp, mp + 1 - 2 * (mp % 2))
    return across_x, across_y, core


def meet(devices):
    barrier = pltpu.get_barrier_semaphore()
    for device in devices:
        pl.semaphore_signal(barrier, inc=1, device_id=device, device_id_type=MESH)
    pl.semaphore_wait(barrier, len(devices))


def gather_kernel(chunks, rows, keys, got_rows, got_keys, send, recv):
    across_x, across_y, core = neighbours()
    meet((across_x, across_y, core))

    def copies(leg, index, source_rows, source_keys, slot, device):
        _, start, length = chunks[index]
        span = pl.ds(start, length)
        return [
            pltpu.make_async_remote_copy(
                src_ref=source.at[span],
                dst_ref=target.at[slot, span],
                send_sem=send.at[leg, index, which],
                recv_sem=recv.at[leg, index, which],
                device_id=device,
                device_id_type=MESH,
            )
            for which, (source, target) in enumerate(
                ((source_rows, got_rows), (source_keys, got_keys))
            )
        ]

    outward, inward, relayed = [], [], []
    for index, (half, _, _) in enumerate(chunks):
        device = across_x if half else across_y
        outward.append(copies(1, index, rows, keys, 1, device))
        for copy in outward[-1]:
            copy.start()
    for index in range(len(chunks)):
        inward.append(copies(0, index, rows, keys, 0, core))
        for copy in inward[-1]:
            copy.start()
    for index in range(len(chunks)):
        for copy in outward[index]:
            copy.wait_recv()
        relayed.append(copies(2, index, got_rows.at[1], got_keys.at[1], 2, core))
        for copy in relayed[-1]:
            copy.start()
    for group in outward:
        for copy in group:
            copy.wait_send()
    for group in inward + relayed:
        for copy in group:
            copy.wait()


def gather(chunks, rows, keys):
    any_space = pl.BlockSpec(memory_space=pl.ANY)
    return pl.pallas_call(
        functools.partial(gather_kernel, chunks),
        out_shape=(
            jax.ShapeDtypeStruct((3,) + rows.shape, rows.dtype),
            jax.ShapeDtypeStruct((3,) + keys.shape, keys.dtype),
        ),
        in_specs=[any_space] * 2,
        out_specs=(any_space,) * 2,
        scratch_shapes=[
            pltpu.SemaphoreType.DMA((3, len(chunks), 2)),
            pltpu.SemaphoreType.DMA((3, len(chunks), 2)),
        ],
        compiler_params=pltpu.CompilerParams(collective_id=0, has_side_effects=True),
    )(rows, keys)


def sum_kernel(wanted, rows, keys, got_rows, got_keys, out):
    want = wanted[0]

    def part(key_row, row_block):
        onehot = jnp.where(want == key_row, 1.0, 0.0).astype(jnp.bfloat16)
        return jnp.dot(onehot, row_block, preferred_element_type=jnp.float32)

    total = part(keys[0], rows[0])
    for slot in range(3):
        total = total + part(got_keys[slot, 0], got_rows[slot, 0])
    out[0] = total.astype(out.dtype)


def sum_rows(cut, wanted, rows, keys, got_rows, got_keys):
    table_count, batch_rows, width = rows.shape
    targets = wanted.shape[1]
    return pl.pallas_call(
        sum_kernel,
        grid=(table_count,),
        out_shape=jax.ShapeDtypeStruct((table_count, targets, width), jnp.bfloat16),
        in_specs=[
            pl.BlockSpec((1, targets, 1), lambda t: (jnp.where(t >= cut, 1, 0), 0, 0)),
            pl.BlockSpec((1, batch_rows, width), lambda t: (t, 0, 0)),
            pl.BlockSpec((1, 1, batch_rows), lambda t: (t, 0, 0)),
            pl.BlockSpec((3, 1, batch_rows, width), lambda t: (0, t, 0, 0)),
            pl.BlockSpec((3, 1, 1, batch_rows), lambda t: (0, t, 0, 0)),
        ],
        out_specs=pl.BlockSpec((1, targets, width), lambda t: (t, 0, 0)),
    )(wanted, rows, keys, got_rows, got_keys)


def scatter_kernel(chunks, z_count, partial, out, first, mixed, last, send1, recv1, send2, recv2):
    across_x, across_y, _ = neighbours()
    dp, mp = lax.axis_index("dp"), lax.axis_index("mp")
    z = dp // 2
    my_side = (mp // 2, dp % 2)
    rows_own = out.shape[1]
    z_devices = [(((z + d) % z_count) * 2 + dp % 2, mp) for d in range(1, z_count)]
    meet([across_x, across_y] + z_devices)

    swaps = []
    for index, (half, start, length) in enumerate(chunks):
        span = pl.ds(start, length)
        other = 1 - (my_side[0] if half else my_side[1])
        swaps.append(
            pltpu.make_async_remote_copy(
                src_ref=partial.at[span, other],
                dst_ref=first.at[span],
                send_sem=send1.at[index],
                recv_sem=recv1.at[index],
                device_id=across_y if half else across_x,
                device_id_type=MESH,
            )
        )
        swaps[-1].start()
    spread = []
    for index, (half, start, length) in enumerate(chunks):
        mine = my_side[0] if half else my_side[1]
        swaps[index].wait_recv()

        def add(step, carry, start=start, mine=mine):
            t = start + step
            total = partial[t, mine].astype(jnp.float32) + first[t].astype(jnp.float32)
            total = total.astype(jnp.bfloat16)
            for owner in range(z_count):
                mixed[owner, t] = total[owner * rows_own : (owner + 1) * rows_own]
            return carry

        lax.fori_loop(0, length, add, 0)
        span = pl.ds(start, length)
        group = []
        for d in range(1, z_count):
            copy = pltpu.make_async_remote_copy(
                src_ref=mixed.at[(z + d) % z_count, span],
                dst_ref=last.at[d - 1, span],
                send_sem=send2.at[index, d - 1],
                recv_sem=recv2.at[index, d - 1],
                device_id=z_devices[d - 1],
                device_id_type=MESH,
            )
            copy.start()
            group.append(copy)
        spread.append(group)
    for index, (half, start, length) in enumerate(chunks):
        for copy in spread[index]:
            copy.wait_recv()

        def finish(step, carry, start=start):
            t = start + step
            total = mixed[z, t].astype(jnp.float32)
            for d in range(1, z_count):
                total = total + last[d - 1, t].astype(jnp.float32)
            out[t] = total
            return carry

        lax.fori_loop(0, length, finish, 0)
    for index in range(len(chunks)):
        swaps[index].wait_send()
        for copy in spread[index]:
            copy.wait_send()


def scatter(chunks, z_count, rows_own, partial):
    table_count, _, side_rows, width = partial.shape
    vmem = pl.BlockSpec(memory_space=pltpu.VMEM)
    count = len(chunks)
    return pl.pallas_call(
        functools.partial(scatter_kernel, chunks, z_count),
        out_shape=jax.ShapeDtypeStruct((table_count, rows_own, width), jnp.float32),
        in_specs=[vmem],
        out_specs=vmem,
        scratch_shapes=[
            pltpu.VMEM((table_count, side_rows, width), jnp.bfloat16),
            pltpu.VMEM((z_count, table_count, rows_own, width), jnp.bfloat16),
            pltpu.VMEM((max(1, z_count - 1), table_count, rows_own, width), jnp.bfloat16),
            pltpu.SemaphoreType.DMA((count,)),
            pltpu.SemaphoreType.DMA((count,)),
            pltpu.SemaphoreType.DMA((count, max(1, z_count - 1))),
            pltpu.SemaphoreType.DMA((count, max(1, z_count - 1))),
        ],
        compiler_params=pltpu.CompilerParams(
            collective_id=1, has_side_effects=True, vmem_limit_bytes=VMEM_LIMIT
        ),
    )(partial)


def wanted_rows(z_count, rows_own, rows_group):
    dp, mp = lax.axis_index("dp"), lax.axis_index("mp")
    side = np.arange(2)[:, None, None]
    z = np.arange(z_count)[None, :, None]
    row = np.arange(rows_own)[None, None, :]
    by_x = jnp.asarray((z * 2 + side) * rows_group + row, jnp.int32) + mp * rows_own
    by_y = (
        jnp.asarray(z * 2 * rows_group + side * 2 * rows_own + row, jnp.int32)
        + (dp % 2) * rows_group
        + (mp % 2) * rows_own
    )
    return jnp.stack([by_x.reshape(-1, 1), by_y.reshape(-1, 1)])


def per_device(sparse_vecs, dense_vec, top_cot, top_weight, owner_ids, local_rows, table, accum):
    batch_rows, table_count, row_width = sparse_vecs.shape
    feature_count = table_count + 1
    rows_own = table.shape[1]
    rows_group = lax.axis_size("mp") * rows_own
    z_count = lax.axis_size("dp") // 2
    cut, chunks = table_chunks(table_count)
    keys = (owner_ids[:, :, 0] * rows_group + local_rows).T[:, None, :]
    input_cot = jnp.einsum("bh,zh->bz", top_cot, top_weight, preferred_element_type=jnp.float32)
    symmetric = jnp.dot(
        input_cot[:, row_width:],
        pair_matrix(feature_count),
        precision=lax.Precision.HIGHEST,
        preferred_element_type=jnp.float32,
    )
    symmetric = symmetric.reshape(batch_rows, feature_count, feature_count)
    features = jnp.concatenate([dense_vec[:, None, :], sparse_vecs], axis=1).astype(jnp.float32)
    feature_grad = jnp.einsum("bij,bje->bie", symmetric, features, precision=lax.Precision.HIGHEST)
    dense_grad = (input_cot[:, :row_width] + feature_grad[:, 0]).astype(jnp.bfloat16)
    rows = feature_grad[:, 1:].astype(jnp.bfloat16).transpose(1, 0, 2)
    got_rows, got_keys = gather(chunks, rows, keys)
    wanted = wanted_rows(z_count, rows_own, rows_group)
    partial = sum_rows(cut, wanted, rows, keys, got_rows, got_keys)
    partial = partial.reshape(table_count, 2, z_count * rows_own, row_width)
    row_grad = scatter(chunks, z_count, rows_own, partial)
    new_accum = accum + jnp.mean(row_grad * row_grad, axis=-1)
    new_table = table - LEARN_RATE * row_grad / (jnp.sqrt(new_accum)[:, :, None] + EPSILON)
    return (dense_grad, new_table, new_accum)


def solution(mesh):
    in_specs = (
        P(("dp", "mp"), None, None),
        P(("dp", "mp"), None),
        P(("dp", "mp"), None),
        P(),
        P(("dp", "mp"), None, None),
        P(("dp", "mp"), None),
        P(None, ("dp", "mp"), None),
        P(None, ("dp", "mp")),
    )
    out_specs = (P(("dp", "mp"), None), P(None, ("dp", "mp"), None), P(None, ("dp", "mp")))
    return jax.shard_map(
        per_device, mesh=mesh, in_specs=in_specs, out_specs=out_specs, check_vma=False
    )
```

time: 366 us -> 108 us (0.30)
  local copies, waits for them, and re-layouts: 163 us -> 17 us
  waiting for transfers between devices: 96.3 us -> 0 us
  Pallas kernels: 0 us -> 77.2 us
  matrix products: 64.4 us -> 8.01 us
  between operations: 14.3 us -> 0.84 us
  starting transfers between devices: 13.3 us -> 0 us
  other arithmetic: 13.5 us -> 4.5 us
    gather x2 -> x0, local copies, waits for them, and re-layouts: 120 us -> none  [the longest x1 73.7 us: per_device(): send_keys = jnp.where(filled, jnp.take(column, safe_source, axis=0), -1)]
    pallas_call x0 -> x3, Pallas kernels: none -> 77.2 us  [the longest x1 31 us: scatter(): pl.pallas_call(functools.partial(scatter_kernel, chunks, z_count), out_sh...]
    all_to_all x2 -> x0, waiting for transfers between devices: 75.7 us -> none  [the longest x1 75.7 us: per_device(): lax.all_to_all(send_rows, 'dp', split_axis=0, concat_axis=0, tiled=True)]
    dot_general x6 -> x0, matrix products: 56.2 us -> none  [the longest x4 55.8 us: add_block(): lax.dot_general(onehot, row_piece, (((0,), (0,)), ((), ())), preferred_el...]
    scatter x1 -> x0, local copies, waits for them, and re-layouts: 24.9 us -> none  [per_device(): source_of = jnp.full((slot_total,), -1, jnp.int32).at[slot_index].set(jnp...]
    reduce_scatter x1 -> x0, waiting for transfers between devices: 20.7 us -> none  [per_device(): lax.psum_scatter(accumulate(recv_rows, recv_keys, jnp.int32(0), lax.axis_...]
    all_to_all x2 -> x0, starting transfers between devices: 13.3 us -> none  [the longest x1 7.28 us: per_device(): lax.all_to_all(send_keys, 'dp', split_axis=0, concat_axis=0, tiled=True)]
    select_n x3 -> x0, other arithmetic: 7.79 us -> none  [the longest x1 7.05 us: per_device(): send_rows = jnp.where(filled[:, None], send_rows, jnp.zeros_like(send_rows))]
  transfers between devices with their start and end apart: 3 -> 0, of which waited for: 2 -> 0; matrix products, arithmetic and copies ran while one was open for 21% -> 0% of each run, Pallas kernels for 0% -> 0%
where the time goes in v1:
time: 108 us
  Pallas kernels  77.2 us (71%)
  local copies, waits for them, and re-layouts  17 us (16%)
  matrix products  8.01 us (7%)
  other arithmetic  4.5 us (4%)
    pallas_call x1, Pallas kernels, scatter(): pl.pallas_call(functools.partial(scatter_kernel, chunks, z_count), out_sh...  31 us
    pallas_call x1, Pallas kernels, gather(): pl.pallas_call(functools.partial(gather_kernel, chunks), out_shape=(jax.S...  26.6 us
    pallas_call x1, Pallas kernels, sum_rows(): pl.pallas_call(sum_kernel, grid=(table_count,), out_shape=jax.ShapeDtypeS...  19.6 us
    unnamed x24, local copies, waits for them, and re-layouts  8.52 us
    reshape x2, local copies, waits for them, and re-layouts, per_device(): symmetric = symmetric.reshape(batch_rows, feature_count, feature_count)  4.57 us
    dot_general x1, matrix products, per_device(): jnp.einsum('bij,bje->bie', symmetric, features, precision=lax.Precision.H...  4.49 us
    slice x1, local copies, waits for them, and re-layouts, per_device(): rows = feature_grad[:, 1:].astype(jnp.bfloat16).transpose(1, 0, 2)  2.73 us

profile of v1, /device:TPU:0, one launch (start us, length us, event | category | flops | bytes accessed | tf_op | source)
XLA Modules:
  0.0 107.5 jit_solution(10779130290826410511)
XLA Ops:
  0.6 0.0 copy-start
  0.6 0.0 copy-start.2
  0.7 1.2 %copy-done = bf16[479,1024]{1,0:T(8,128)(2,1)S(1)} copy-done((bf16[479,1024]{1,0:T(8,128)(2,1)S(1)}, bf16[479,1024]{1,0:T(8,128)(2,1)}, u32[]{:S(2)}) %copy-start) | copy-done | bytes 981016
  1.8 1.5 %fusion.10 = f32[256,479]{0,1:T(8,128)S(1)} fusion(bf16[256,1024]{1,0:T(8,128)(2,1)} %param.13, bf16[479,1024]{1,0:T(8,128)(2,1)S(1)} %copy-done), kind=kOutput, calls=%fused_computation.21 | convolution fusion | flops 251133952 | bytes 1995776 | tf_op jit(solution)/shard_map/bh,zh->bz/dot_general | solution.py:268
  3.3 0.0 copy-done.2
  3.4 2.0 %fusion.5 = f32[256,729]{0,1:T(8,128)S(1)} fusion(f32[351,729]{1,0:T(8,128)S(1)} %copy-done.2, f32[256,479]{0,1:T(8,128)S(1)} %fusion.10), kind=kOutput, calls=%fused_computation.8 | convolution fusion | flops 786060288 | bytes 2188288 | tf_op jit(solution)/shard_map/dot_general | solution.py:269
  5.4 0.1 reshape.16
  5.5 4.5 %copy.41 = f32[256,27,27]{2,1,0:T(8,128)} copy(f32[256,27,27]{0,2,1:T(8,128)S(1)} %reshape.16) | data formatting | bytes 1492992 | tf_op jit(solution)/shard_map/reshape | solution.py:275
  10.0 0.0 copy-start.4
  10.0 2.6 %copy.40 = bf16[256,26,128]{2,1,0:T(8,128)(2,1)S(1)} copy(bf16[256,26,128]{2,0,1:T(8,128)(2,1)} %param.11) | data formatting | bytes 3407872 | tf_op args[0]
  12.6 0.0 copy-done.4
  12.6 0.1 copy.39
  12.7 0.0 copy-start.8
  12.7 0.0 copy-start.9
  12.7 4.5 %fusion = f32[256,27,128]{2,1,0:T(8,128)S(1)} fusion(f32[256,27,27]{2,1,0:T(8,128)} %copy.41, bf16[256,26,128]{2,1,0:T(8,128)(2,1)S(1)} %copy.40, bf16[256,1,128]{2,1,0:T(2,128)(2,1)S(1)} %copy.39), kind=kOutput, calls=%fused_computation.1 | convolution fusion | flops 290193408 | bytes 6054912 | tf_op jit(solution)/shard_map/bij,bje->bie/dot_general | solution.py:277
  17.2 0.0 copy-start.1
  17.3 1.9 %copy-done.1 = f32[256,27,128]{2,1,0:T(8,128)} copy-done((f32[256,27,128]{2,1,0:T(8,128)}, f32[256,27,128]{2,1,0:T(8,128)S(1)}, u32[]{:S(2)}) %copy-start.1) | copy-done | bytes 3538968
  19.2 0.1 slice.19
  19.3 0.1 copy.48
  19.5 0.7 copy.47
  20.2 0.0 copy-done.8
  20.2 0.1 stack_reshape.9
  20.3 0.0 copy-done.9
  20.4 0.1 stack_reshape.8
  20.5 0.7 pad_add_fusion.wanted
  21.2 2.7 %slice.20 = bf16[256,26,128]{2,1,0:T(8,128)(2,1)S(1)} slice(f32[256,27,128]{2,1,0:T(8,128)} %copy-done.1), slice={[0:256], [1:27], [0:128]} | slice | bytes 3407872 | tf_op jit(solution)/shard_map/slice | solution.py:279
  24.0 0.0 copy-start.5
  24.0 0.0 copy-start.6
  24.0 1.9 %copy.56 = bf16[256,26,128]{2,0,1:T(8,128)(2,1)} copy(bf16[256,26,128]{2,1,0:T(8,128)(2,1)S(1)} %slice.20) | data formatting | bytes 3407872
  25.9 0.0 copy-done.5
  25.9 0.0 copy-done.6
  25.9 0.6 broadcast_in_dim.8.keys
  26.5 26.6 %shard_map.130 = (bf16[3,26,256,128]{3,2,1,0:T(8,128)(2,1)}, s32[3,26,1,256]{3,2,1,0:T(1,128)}) custom-call(bf16[26,256,128]{2,1,0:T(8,128)(2,1)} %bitcast.23, s32[26,1,256]{2,1,0:T(1,128)} %broadcast_in_dim.8.keys), custom_call_target="tpu_custom_call" | custom-call | tf_op jit(solution)/shard_map/pallas_call | solution.py:104
  53.2 19.6 %shard_map.131 = bf16[26,256,128]{2,1,0:T(8,128)(2,1)} custom-call(s32[2,256,1]{2,1,0:T(8,128)} %pad_add_fusion.wanted, bf16[26,256,128]{2,1,0:T(8,128)(2,1)} %bitcast.24, s32[26,1,256]{2,1,0:T(1,128)} %broadcast_in_dim.8.keys, bf16[3,26,256,128]{3,2,1,0:T(8,128)(2,1)} %get-tuple-element.5.got_rows, s32[3,26,1,256]{3,2,1,0:T(1,128)} %get-tuple-element.6.got_keys), custom_call_target="tpu_custom_call" | custom-call | tf_op jit(solution)/shard_map/pallas_call | solution.py:136
  72.8 0.0 copy-start.7
  72.8 0.0 copy-start.3
  72.8 31.0 %shard_map.132 = f32[26,32,128]{2,1,0:T(8,128)} custom-call(bf16[26,2,128,128]{3,2,1,0:T(8,128)(2,1)} %bitcast.25), custom_call_target="tpu_custom_call" | custom-call | tf_op jit(solution)/shard_map/pallas_call | solution.py:226
  103.8 1.2 %multiply_reduce_fusion = f32[26,32]{1,0:T(8,128)S(1)} fusion(f32[26,32,128]{2,1,0:T(8,128)} %shard_map.132), kind=kLoop, calls=%fused_computation.7 | loop fusion | flops 212160 | bytes 429312 | tf_op jit(solution)/shard_map/reduce_sum | solution.py:285
  105.0 0.0 copy-done.7
  105.0 0.6 sqrt_add_fusion
  105.6 0.0 copy-done.3
  105.6 1.9 %divide_subtract_fusion = f32[26,32,128]{2,1,0:T(8,128)} fusion(f32[26,32,128]{2,1,0:T(8,128)S(1)} %copy-done.3, f32[26,32,128]{2,1,0:T(8,128)} %shard_map.132, f32[26,32]{1,0:T(8,128)S(1)} %get-tuple-element.19), kind=kLoop, calls=%fused_computation.6 | loop fusion | flops 319488 | bytes 1281280 | tf_op jit(solution)/shard_map/sub | solution.py:286
  (4 shorter events, 0.0 us)
Async XLA Ops:
  0.6 1.2 %copy-start = (bf16[479,1024]{1,0:T(8,128)(2,1)S(1)}, bf16[479,1024]{1,0:T(8,128)(2,1)}, u32[]{:S(2)}) copy-start(bf16[479,1024]{1,0:T(8,128)(2,1)} %param.14) | copy-start | bytes 2942980
  0.6 2.7 %copy-start.2 = (f32[351,729]{1,0:T(8,128)S(1)}, f32[351,729]{1,0:T(8,128)}, u32[]{:S(2)}) copy-start(f32[351,729]{1,0:T(8,128)} %constant.46.clone) | copy-start | bytes 3070552
  10.0 2.6 %copy-start.4 = (bf16[256,128]{1,0:T(8,128)(2,1)S(1)}, bf16[256,128]{1,0:T(8,128)(2,1)}, u32[]{:S(2)}) copy-start(bf16[256,128]{1,0:T(8,128)(2,1)} %param.12) | copy-start | bytes 196612
  12.7 7.5 %copy-start.8 = (s32[2,4,32]{2,1,0:T(4,128)S(1)}, s32[2,4,32]{2,1,0:T(4,128)}, u32[]{:S(2)}) copy-start(s32[2,4,32]{2,1,0:T(4,128)} %constant.48.clone) | copy-start | bytes 3076
  12.7 7.6 %copy-start.9 = (s32[2,4,32]{2,1,0:T(4,128)S(1)}, s32[2,4,32]{2,1,0:T(4,128)}, u32[]{:S(2)}) copy-start(s32[2,4,32]{2,1,0:T(4,128)} %constant.47.clone) | copy-start | bytes 3076
  17.2 1.9 %copy-start.1 = (f32[256,27,128]{2,1,0:T(8,128)}, f32[256,27,128]{2,1,0:T(8,128)S(1)}, u32[]{:S(2)}) copy-start(f32[256,27,128]{2,1,0:T(8,128)S(1)} %fusion) | copy-start | bytes 10616836
  24.0 1.9 %copy-start.5 = (s32[256,26]{0,1:T(8,128)S(1)}, s32[256,26]{0,1:T(8,128)}, u32[]{:S(2)}) copy-start(s32[256,26]{0,1:T(8,128)} %param.16) | copy-start | bytes 79876
  24.0 1.9 %copy-start.6 = (s32[256,26,1]{0,2,1:T(1,128)S(1)}, s32[256,26,1]{0,2,1:T(1,128)}, u32[]{:S(2)}) copy-start(s32[256,26,1]{0,2,1:T(1,128)} %param.15) | copy-start | bytes 79876
  72.8 32.2 %copy-start.7 = (f32[26,32]{1,0:T(8,128)S(1)}, f32[26,32]{1,0:T(8,128)}, u32[]{:S(2)}) copy-start(f32[26,32]{1,0:T(8,128)} %param.18) | copy-start | bytes 9988
  72.8 32.8 %copy-start.3 = (f32[26,32,128]{2,1,0:T(8,128)S(1)}, f32[26,32,128]{2,1,0:T(8,128)}, u32[]{:S(2)}) copy-start(f32[26,32,128]{2,1,0:T(8,128)} %param.17) | copy-start | bytes 1277956

commit v2 on v1

v2 whole, which is shorter than its diff:
```python
import functools

import jax
import jax.numpy as jnp
import numpy as np
from jax import lax
from jax.experimental import pallas as pl
from jax.experimental.pallas import tpu as pltpu
from jax.sharding import PartitionSpec as P

LEARN_RATE = 0.1
EPSILON = 1e-08
MESH = pl.DeviceIdType.MESH
CHUNKS = 4
LEAD = 4
VMEM_LIMIT = 60 * 1024 * 1024


def pair_matrix(feature_count):
    row_index, col_index = np.tril_indices(feature_count, -1)
    pair_count = row_index.shape[0]
    matrix = np.zeros((pair_count, feature_count * feature_count), np.float32)
    matrix[np.arange(pair_count), row_index * feature_count + col_index] = 1.0
    matrix[np.arange(pair_count), col_index * feature_count + row_index] = 1.0
    return jnp.asarray(matrix)


def table_chunks(table_count):
    cut = (table_count + 1) // 2
    halves = []
    for half, (low, high) in enumerate(((0, cut), (cut, table_count))):
        edges = [low + (high - low) * k // CHUNKS for k in range(CHUNKS + 1)]
        halves.append([(half, a, b - a) for a, b in zip(edges, edges[1:]) if b > a])
    out = []
    for k in range(CHUNKS):
        for pieces in halves:
            if k < len(pieces):
                out.append(pieces[k])
    return cut, out


def neighbours():
    dp, mp = lax.axis_index("dp"), lax.axis_index("mp")
    mp_count = lax.axis_size("mp")
    across_x = (dp + 1 - 2 * (dp % 2), mp)
    across_y = (dp, (mp + mp_count // 2) % mp_count)
    core = (dp, mp + 1 - 2 * (mp % 2))
    return across_x, across_y, core


def meet(devices):
    barrier = pltpu.get_barrier_semaphore()
    for device in devices:
        pl.semaphore_signal(barrier, inc=1, device_id=device, device_id_type=MESH)
    pl.semaphore_wait(barrier, len(devices))


def route_kernel(
    chunks, z_count, rows, keys, out, got_rows, got_keys, partial, first, mixed, last,
    send, recv, send1, recv1, send2, recv2,
):
    across_x, across_y, core = neighbours()
    dp, mp = lax.axis_index("dp"), lax.axis_index("mp")
    z = dp // 2
    my_side = (mp // 2, dp % 2)
    rows_own = out.shape[1]
    side_rows = z_count * rows_own
    bases = (mp * 2 * side_rows, ((mp % 2) * 2 + dp % 2) * 2 * side_rows)
    z_devices = [(((z + d) % z_count) * 2 + dp % 2, mp) for d in range(1, z_count)]
    meet([across_x, across_y, core] + z_devices)
    count = len(chunks)

    def copies(leg, index, source_rows, source_keys, slot, device):
        _, start, length = chunks[index]
        span = pl.ds(start, length)
        return [
            pltpu.make_async_remote_copy(
                src_ref=source.at[span],
                dst_ref=target.at[slot, span],
                send_sem=send.at[leg, index, which],
                recv_sem=recv.at[leg, index, which],
                device_id=device,
                device_id_type=MESH,
            )
            for which, (source, target) in enumerate(
                ((source_rows, got_rows), (source_keys, got_keys))
            )
        ]

    started = []

    def begin(group):
        for copy in group:
            copy.start()
        started.extend(group)
        return group

    outward, inward, relayed, swaps, spread = [], [], [], [], []

    def send_out(index):
        if index < count:
            half = chunks[index][0]
            outward.append(
                begin(copies(1, index, rows, keys, 1, across_x if half else across_y))
            )
            inward.append(begin(copies(0, index, rows, keys, 0, core)))

    def relay(index):
        for copy in outward[index]:
            copy.wait_recv()
        relayed.append(begin(copies(2, index, got_rows.at[1], got_keys.at[1], 2, core)))

    def sums(index):
        half, start, length = chunks[index]
        for copy in inward[index] + relayed[index]:
            copy.wait_recv()
        base = bases[half]
        batch_rows = rows.shape[1]
        targets = lax.broadcasted_iota(jnp.int32, (2 * side_rows, batch_rows), 0)

        def add_table(step, carry):
            t = start + step

            def part(key_row, row_block):
                onehot = jnp.where(targets == key_row - base, 1.0, 0.0).astype(jnp.bfloat16)
                return jnp.dot(onehot, row_block, preferred_element_type=jnp.float32)

            total = part(keys[t], rows[t])
            for slot in range(3):
                total = total + part(got_keys[slot, t], got_rows[slot, t])
            total = total.astype(jnp.bfloat16)
            partial[t, 0] = total[:side_rows]
            partial[t, 1] = total[side_rows:]
            return carry

        lax.fori_loop(0, length, add_table, 0)
        span = pl.ds(start, length)
        other = 1 - (my_side[0] if half else my_side[1])
        swaps.append(
            pltpu.make_async_remote_copy(
                src_ref=partial.at[span, other],
                dst_ref=first.at[span],
                send_sem=send1.at[index],
                recv_sem=recv1.at[index],
                device_id=across_y if half else across_x,
                device_id_type=MESH,
            )
        )
        begin(swaps[-1:])

    def along_z(index):
        half, start, length = chunks[index]
        mine = my_side[0] if half else my_side[1]
        swaps[index].wait_recv()

        def add(step, carry):
            t = start + step
            total = partial[t, mine].astype(jnp.float32) + first[t].astype(jnp.float32)
            total = total.astype(jnp.bfloat16)
            for owner in range(z_count):
                mixed[owner, t] = total[owner * rows_own : (owner + 1) * rows_own]
            return carry

        lax.fori_loop(0, length, add, 0)
        span = pl.ds(start, length)
        group = [
            pltpu.make_async_remote_copy(
                src_ref=mixed.at[(z + d) % z_count, span],
                dst_ref=last.at[d - 1, span],
                send_sem=send2.at[index, d - 1],
                recv_sem=recv2.at[index, d - 1],
                device_id=z_devices[d - 1],
                device_id_type=MESH,
            )
            for d in range(1, z_count)
        ]
        spread.append(begin(group))

    def finish(index):
        _, start, length = chunks[index]
        for copy in spread[index]:
            copy.wait_recv()

        def add(step, carry):
            t = start + step
            total = mixed[z, t].astype(jnp.float32)
            for d in range(1, z_count):
                total = total + last[d - 1, t].astype(jnp.float32)
            out[t] = total
            return carry

        lax.fori_loop(0, length, add, 0)

    for index in range(LEAD):
        send_out(index)
    for index in range(count + 3):
        if index < count:
            relay(index)
            send_out(index + LEAD)
        if 0 <= index - 1 < count:
            sums(index - 1)
        if 0 <= index - 3 < count:
            along_z(index - 3)
    for index in range(count):
        finish(index)
    for copy in started:
        copy.wait_send()


def route(chunks, z_count, rows_own, rows, keys):
    table_count, batch_rows, width = rows.shape
    side_rows = z_count * rows_own
    others = max(1, z_count - 1)
    vmem = pl.BlockSpec(memory_space=pltpu.VMEM)
    count = len(chunks)
    return pl.pallas_call(
        functools.partial(route_kernel, chunks, z_count),
        out_shape=jax.ShapeDtypeStruct((table_count, rows_own, width), jnp.float32),
        in_specs=[vmem] * 2,
        out_specs=vmem,
        scratch_shapes=[
            pltpu.VMEM((3,) + rows.shape, rows.dtype),
            pltpu.VMEM((3,) + keys.shape, keys.dtype),
            pltpu.VMEM((table_count, 2, side_rows, width), jnp.bfloat16),
            pltpu.VMEM((table_count, side_rows, width), jnp.bfloat16),
            pltpu.VMEM((z_count, table_count, rows_own, width), jnp.bfloat16),
            pltpu.VMEM((others, table_count, rows_own, width), jnp.bfloat16),
            pltpu.SemaphoreType.DMA((3, count, 2)),
            pltpu.SemaphoreType.DMA((3, count, 2)),
            pltpu.SemaphoreType.DMA((count,)),
            pltpu.SemaphoreType.DMA((count,)),
            pltpu.SemaphoreType.DMA((count, others)),
            pltpu.SemaphoreType.DMA((count, others)),
        ],
        compiler_params=pltpu.CompilerParams(
            collective_id=0, has_side_effects=True, vmem_limit_bytes=VMEM_LIMIT
        ),
    )(rows, keys)


def encode_keys(cut, z_count, rows_own, owner, local):
    x, z = owner % 2, owner // 2
    mp, row = local // rows_own, local % rows_own
    y, core = mp // 2, mp % 2
    place = z * rows_own + row
    by_x = (mp * 2 + x) * (z_count * rows_own) + place
    by_y = ((core * 2 + x) * 2 + y) * (z_count * rows_own) + place
    first_half = jnp.arange(owner.shape[1])[None, :] < cut
    return jnp.where(first_half, by_x, by_y).T[:, None, :]


def per_device(sparse_vecs, dense_vec, top_cot, top_weight, owner_ids, local_rows, table, accum):
    batch_rows, table_count, row_width = sparse_vecs.shape
    feature_count = table_count + 1
    rows_own = table.shape[1]
    z_count = lax.axis_size("dp") // 2
    cut, chunks = table_chunks(table_count)
    keys = encode_keys(cut, z_count, rows_own, owner_ids[:, :, 0], local_rows)
    input_cot = jnp.einsum("bh,zh->bz", top_cot, top_weight, preferred_element_type=jnp.float32)
    symmetric = jnp.dot(
        input_cot[:, row_width:].astype(jnp.bfloat16),
        pair_matrix(feature_count).astype(jnp.bfloat16),
        preferred_element_type=jnp.bfloat16,
    )
    symmetric = symmetric.reshape(batch_rows, feature_count, feature_count)
    features = jnp.concatenate([dense_vec[:, None, :], sparse_vecs], axis=1)
    feature_grad = jnp.einsum(
        "bij,bje->bie", symmetric, features, preferred_element_type=jnp.float32
    )
    dense_grad = (input_cot[:, :row_width] + feature_grad[:, 0]).astype(jnp.bfloat16)
    rows = feature_grad[:, 1:].astype(jnp.bfloat16).transpose(1, 0, 2)
    row_grad = route(chunks, z_count, rows_own, rows, keys)
    new_accum = accum + jnp.mean(row_grad * row_grad, axis=-1)
    new_table = table - LEARN_RATE * row_grad / (jnp.sqrt(new_accum)[:, :, None] + EPSILON)
    return (dense_grad, new_table, new_accum)


def solution(mesh):
    in_specs = (
        P(("dp", "mp"), None, None),
        P(("dp", "mp"), None),
        P(("dp", "mp"), None),
        P(),
        P(("dp", "mp"), None, None),
        P(("dp", "mp"), None),
        P(None, ("dp", "mp"), None),
        P(None, ("dp", "mp")),
    )
    out_specs = (P(("dp", "mp"), None), P(None, ("dp", "mp"), None), P(None, ("dp", "mp")))
    return jax.shard_map(
        per_device, mesh=mesh, in_specs=in_specs, out_specs=out_specs, check_vma=False
    )
```

time: 108 us -> 70.8 us (0.66)
  Pallas kernels: 77.2 us -> 48.9 us
  matrix products: 8.01 us -> 2.67 us
  local copies, waits for them, and re-layouts: 17 us -> 13.3 us
    pallas_call x3 -> x1, Pallas kernels: 77.2 us -> 48.9 us  [route(): pl.pallas_call(functools.partial(route_kernel, chunks, z_count), out_shap...]
    dot_general x2, matrix products: 6.51 us -> 1.18 us  [the longest x1 0.77 us: per_device(): jnp.einsum('bij,bje->bie', symmetric, features, preferred_element_type=jn...]
    slice x1, local copies, waits for them, and re-layouts: 2.73 us -> 0.56 us  [per_device(): rows = feature_grad[:, 1:].astype(jnp.bfloat16).transpose(1, 0, 2)]
    reshape x2, local copies, waits for them, and re-layouts: 4.57 us -> 3.32 us  [per_device(): symmetric = symmetric.reshape(batch_rows, feature_count, feature_count)]
    slice x1, local copies, waits for them, and re-layouts: 0.14 us -> 1.29 us  [per_device(): feature_grad[:, 0]]
    unnamed x24 -> x22, local copies, waits for them, and re-layouts: 8.52 us -> 7.39 us
where the time goes in v2:
time: 70.8 us; the launch traced here: 70.4 us
  Pallas kernels  48.9 us (69%)
  local copies, waits for them, and re-layouts  13.3 us (19%)
  other arithmetic  4.78 us (7%)
  matrix products  2.67 us (4%)
  between operations  0.81 us (1%)
    pallas_call x1, Pallas kernels, route(): pl.pallas_call(functools.partial(route_kernel, chunks, z_count), out_shap...  48.9 us
    unnamed x22, local copies, waits for them, and re-layouts  7.39 us
    reshape x2, local copies, waits for them, and re-layouts, per_device(): symmetric = symmetric.reshape(batch_rows, feature_count, feature_count)  3.32 us
    sub x1, other arithmetic, per_device(): table - LEARN_RATE * row_grad / (jnp.sqrt(new_accum)[:, :, None] + EPSILON)  1.95 us
    dot_general x1, matrix products, per_device(): jnp.einsum('bh,zh->bz', top_cot, top_weight, preferred_element_type=jnp.f...  1.5 us

profile of v2, /device:TPU:0, one launch (start us, length us, event | category | flops | bytes accessed | tf_op | source)
XLA Modules:
  0.0 70.4 jit_solution(6307758371653127646)
XLA Ops:
  0.6 0.0 copy-start
  0.6 0.0 copy-start.3
  0.7 1.2 %copy-done = bf16[479,1024]{1,0:T(8,128)(2,1)S(1)} copy-done((bf16[479,1024]{1,0:T(8,128)(2,1)S(1)}, bf16[479,1024]{1,0:T(8,128)(2,1)}, u32[]{:S(2)}) %copy-start) | copy-done | bytes 981016
  1.8 1.5 %fusion.29 = f32[256,479]{0,1:T(8,128)S(1)} fusion(bf16[256,1024]{1,0:T(8,128)(2,1)} %param.11, bf16[479,1024]{1,0:T(8,128)(2,1)S(1)} %copy-done), kind=kOutput, calls=%fused_computation.56 | convolution fusion | flops 251133952 | bytes 1995776 | tf_op jit(solution)/shard_map/bh,zh->bz/dot_general | solution.py:259
  3.3 0.0 copy-start.2
  3.4 0.8 %copy-done.2 = f32[256,479]{0,1:T(8,128)} copy-done((f32[256,479]{0,1:T(8,128)}, f32[256,479]{0,1:T(8,128)S(1)}, u32[]{:S(2)}) %copy-start.2) | copy-done | bytes 490520
  4.1 0.0 copy-done.3
  4.1 0.4 fusion.5
  4.5 0.1 reshape.16
  4.7 3.2 %copy.19 = bf16[256,27,27]{2,1,0:T(8,128)(2,1)S(1)} copy(bf16[256,27,27]{0,2,1:T(8,128)(2,1)S(1)} %reshape.16) | data formatting | bytes 746496 | tf_op jit(solution)/shard_map/reshape | solution.py:265
  7.9 0.0 copy-start.5
  7.9 2.6 %copy.18 = bf16[256,26,128]{2,1,0:T(8,128)(2,1)S(1)} copy(bf16[256,26,128]{2,0,1:T(8,128)(2,1)} %param.9) | data formatting | bytes 3407872 | tf_op args[0]
  10.5 0.0 copy-done.5
  10.5 0.1 copy.17
  10.6 0.8 %fusion = f32[256,27,128]{2,1,0:T(8,128)S(1)} fusion(bf16[256,27,27]{2,1,0:T(8,128)(2,1)S(1)} %copy.19, bf16[256,26,128]{2,1,0:T(8,128)(2,1)S(1)} %copy.18, bf16[256,1,128]{2,1,0:T(2,128)(2,1)S(1)} %copy.17), kind=kOutput, calls=%fused_computation.1 | convolution fusion | flops 51314688 | bytes 5681664 | tf_op jit(solution)/shard_map/bij,bje->bie/dot_general | solution.py:267
  11.4 0.0 copy-start.1
  11.4 0.6 slice.21
  12.0 0.0 copy-start.6
  12.0 0.0 copy-start.7
  12.0 1.9 %copy.48 = bf16[256,26,128]{2,0,1:T(8,128)(2,1)} copy(bf16[256,26,128]{2,1,0:T(8,128)(2,1)S(1)} %slice.21) | data formatting | bytes 3407872
  14.0 0.0 copy-done.1
  14.0 0.0 copy-start.8
  14.0 0.0 copy-start.4
  14.0 0.0 copy-done.6
  14.0 0.0 copy-done.7
  14.0 0.1 fusion.16
  14.1 0.6 broadcast_in_dim.18.keys
  14.7 48.9 %shard_map.112 = f32[26,32,128]{2,1,0:T(8,128)} custom-call(bf16[26,256,128]{2,1,0:T(8,128)(2,1)} %bitcast.34, s32[26,1,256]{2,1,0:T(1,128)} %broadcast_in_dim.18.keys), custom_call_target="tpu_custom_call" | custom-call | tf_op jit(solution)/shard_map/pallas_call | solution.py:216
  63.6 1.2 %multiply_reduce_fusion = f32[26,32]{1,0:T(8,128)S(1)} fusion(f32[26,32,128]{2,1,0:T(8,128)} %shard_map.112), kind=kLoop, calls=%fused_computation.7 | loop fusion | flops 212160 | bytes 429312 | tf_op jit(solution)/shard_map/reduce_sum | solution.py:273
  64.8 0.0 copy-done.8
  64.8 0.6 sqrt_add_fusion
  65.4 0.0 copy-done.4
  65.4 1.9 %divide_subtract_fusion = f32[26,32,128]{2,1,0:T(8,128)} fusion(f32[26,32,128]{2,1,0:T(8,128)S(1)} %copy-done.4, f32[26,32,128]{2,1,0:T(8,128)} %shard_map.112, f32[26,32]{1,0:T(8,128)S(1)} %get-tuple-element.9), kind=kLoop, calls=%fused_computation.6 | loop fusion | flops 319488 | bytes 1281280 | tf_op jit(solution)/shard_map/sub | solution.py:274
  67.4 1.3 %slice.20 = f32[256,1,128]{2,1,0:T(1,128)S(1)} slice(f32[256,27,128]{2,1,0:T(8,128)} %copy-done.1), slice={[0:256], [0:1], [0:128]} | slice | bytes 262144 | tf_op jit(solution)/shard_map/slice | solution.py:270
  68.7 0.1 copy.24
  68.8 0.9 %fusion.6 = bf16[256,128]{0,1:T(8,128)(2,1)S(1)} fusion(f32[256,479]{0,1:T(8,128)} %copy-done.2, f32[256,1,128]{0,2,1:T(8,128)S(1)} %copy.24), kind=kLoop, calls=%fused_computation.11 | loop fusion | flops 65536 | bytes 327680 | tf_op jit(solution)/shard_map/convert_element_type | solution.py:270
  69.7 0.7 %copy.22 = bf16[256,128]{1,0:T(8,128)(2,1)} copy(bf16[256,128]{0,1:T(8,128)(2,1)S(1)} %fusion.6) | data formatting | bytes 131072
  (1 shorter events, 0.0 us)
Async XLA Ops:
  0.6 1.2 %copy-start = (bf16[479,1024]{1,0:T(8,128)(2,1)S(1)}, bf16[479,1024]{1,0:T(8,128)(2,1)}, u32[]{:S(2)}) copy-start(bf16[479,1024]{1,0:T(8,128)(2,1)} %param.12) | copy-start | bytes 2942980
  0.6 3.5 %copy-start.3 = (bf16[351,729]{1,0:T(8,128)(2,1)S(1)}, bf16[351,729]{1,0:T(8,128)(2,1)}, u32[]{:S(2)}) copy-start(bf16[351,729]{1,0:T(8,128)(2,1)} %constant.76) | copy-start | bytes 1535278
  3.3 0.8 %copy-start.2 = (f32[256,479]{0,1:T(8,128)}, f32[256,479]{0,1:T(8,128)S(1)}, u32[]{:S(2)}) copy-start(f32[256,479]{0,1:T(8,128)S(1)} %fusion.29) | copy-start | bytes 1471492
  7.9 2.7 %copy-start.5 = (bf16[256,128]{1,0:T(8,128)(2,1)S(1)}, bf16[256,128]{1,0:T(8,128)(2,1)}, u32[]{:S(2)}) copy-start(bf16[256,128]{1,0:T(8,128)(2,1)} %param.10) | copy-start | bytes 196612
  11.4 2.5 %copy-start.1 = (f32[256,27,128]{2,1,0:T(8,128)}, f32[256,27,128]{2,1,0:T(8,128)S(1)}, u32[]{:S(2)}) copy-start(f32[256,27,128]{2,1,0:T(8,128)S(1)} %fusion) | copy-start | bytes 10616836
  12.0 2.0 %copy-start.6 = (s32[256,26]{0,1:T(8,128)S(1)}, s32[256,26]{0,1:T(8,128)}, u32[]{:S(2)}) copy-start(s32[256,26]{0,1:T(8,128)} %param.14) | copy-start | bytes 79876
  12.0 2.0 %copy-start.7 = (s32[256,26,1]{0,2,1:T(1,128)S(1)}, s32[256,26,1]{0,2,1:T(1,128)}, u32[]{:S(2)}) copy-start(s32[256,26,1]{0,2,1:T(1,128)} %param.13) | copy-start | bytes 79876
  14.0 50.9 %copy-start.8 = (f32[26,32]{1,0:T(8,128)S(1)}, f32[26,32]{1,0:T(8,128)}, u32[]{:S(2)}) copy-start(f32[26,32]{1,0:T(8,128)} %param.16) | copy-start | bytes 9988
  14.0 51.5 %copy-start.4 = (f32[26,32,128]{2,1,0:T(8,128)S(1)}, f32[26,32,128]{2,1,0:T(8,128)}, u32[]{:S(2)}) copy-start(f32[26,32,128]{2,1,0:T(8,128)} %param.15) | copy-start | bytes 1277956

commit v3 on v2

--- a/solution.py
+++ b/solution.py
@@ -11,7 +11,7 @@
 LEARN_RATE = 0.1
 EPSILON = 1e-08
 MESH = pl.DeviceIdType.MESH
-CHUNKS = 4
+CHUNKS = 6
 LEAD = 4
 VMEM_LIMIT = 60 * 1024 * 1024
 

time: 70.8 us -> 70 us (0.989)
  Pallas kernels: 48.9 us -> 48.1 us
    pallas_call x1, Pallas kernels: 48.9 us -> 48.1 us  [route(): pl.pallas_call(functools.partial(route_kernel, chunks, z_count), out_shap...]
where the time goes in v3:
time: 70 us; the launch traced here: 69.6 us
  Pallas kernels  48.1 us (69%)
  local copies, waits for them, and re-layouts  13.3 us (19%)
  other arithmetic  4.78 us (7%)
  matrix products  2.67 us (4%)
  between operations  0.81 us (1%)
    pallas_call x1, Pallas kernels, route(): pl.pallas_call(functools.partial(route_kernel, chunks, z_count), out_shap...  48.1 us
    unnamed x22, local copies, waits for them, and re-layouts  7.39 us
    reshape x2, local copies, waits for them, and re-layouts, per_device(): symmetric = symmetric.reshape(batch_rows, feature_count, feature_count)  3.32 us
    sub x1, other arithmetic, per_device(): table - LEARN_RATE * row_grad / (jnp.sqrt(new_accum)[:, :, None] + EPSILON)  1.95 us
    dot_general x1, matrix products, per_device(): jnp.einsum('bh,zh->bz', top_cot, top_weight, preferred_element_type=jnp.f...  1.5 us

profile of v3, /device:TPU:0, one launch (start us, length us, event | category | flops | bytes accessed | tf_op | source)
XLA Modules:
  0.0 69.6 jit_solution(7841515104360677797)
XLA Ops:
  0.6 0.0 copy-start
  0.6 0.0 copy-start.3
  0.7 1.2 %copy-done = bf16[479,1024]{1,0:T(8,128)(2,1)S(1)} copy-done((bf16[479,1024]{1,0:T(8,128)(2,1)S(1)}, bf16[479,1024]{1,0:T(8,128)(2,1)}, u32[]{:S(2)}) %copy-start) | copy-done | bytes 981016
  1.8 1.5 %fusion.29 = f32[256,479]{0,1:T(8,128)S(1)} fusion(bf16[256,1024]{1,0:T(8,128)(2,1)} %param.11, bf16[479,1024]{1,0:T(8,128)(2,1)S(1)} %copy-done), kind=kOutput, calls=%fused_computation.56 | convolution fusion | flops 251133952 | bytes 1995776 | tf_op jit(solution)/shard_map/bh,zh->bz/dot_general | solution.py:259
  3.3 0.0 copy-start.2
  3.4 0.8 %copy-done.2 = f32[256,479]{0,1:T(8,128)} copy-done((f32[256,479]{0,1:T(8,128)}, f32[256,479]{0,1:T(8,128)S(1)}, u32[]{:S(2)}) %copy-start.2) | copy-done | bytes 490520
  4.1 0.0 copy-done.3
  4.1 0.4 fusion.5
  4.5 0.1 reshape.16
  4.7 3.2 %copy.19 = bf16[256,27,27]{2,1,0:T(8,128)(2,1)S(1)} copy(bf16[256,27,27]{0,2,1:T(8,128)(2,1)S(1)} %reshape.16) | data formatting | bytes 746496 | tf_op jit(solution)/shard_map/reshape | solution.py:265
  7.9 0.0 copy-start.5
  7.9 2.6 %copy.18 = bf16[256,26,128]{2,1,0:T(8,128)(2,1)S(1)} copy(bf16[256,26,128]{2,0,1:T(8,128)(2,1)} %param.9) | data formatting | bytes 3407872 | tf_op args[0]
  10.5 0.0 copy-done.5
  10.5 0.1 copy.17
  10.6 0.8 %fusion = f32[256,27,128]{2,1,0:T(8,128)S(1)} fusion(bf16[256,27,27]{2,1,0:T(8,128)(2,1)S(1)} %copy.19, bf16[256,26,128]{2,1,0:T(8,128)(2,1)S(1)} %copy.18, bf16[256,1,128]{2,1,0:T(2,128)(2,1)S(1)} %copy.17), kind=kOutput, calls=%fused_computation.1 | convolution fusion | flops 51314688 | bytes 5681664 | tf_op jit(solution)/shard_map/bij,bje->bie/dot_general | solution.py:267
  11.4 0.0 copy-start.1
  11.4 0.6 slice.21
  12.0 0.0 copy-start.6
  12.0 0.0 copy-start.7
  12.0 1.9 %copy.48 = bf16[256,26,128]{2,0,1:T(8,128)(2,1)} copy(bf16[256,26,128]{2,1,0:T(8,128)(2,1)S(1)} %slice.21) | data formatting | bytes 3407872
  14.0 0.0 copy-done.1
  14.0 0.0 copy-start.8
  14.0 0.0 copy-start.4
  14.0 0.0 copy-done.6
  14.0 0.0 copy-done.7
  14.0 0.1 fusion.16
  14.1 0.6 broadcast_in_dim.18.keys
  14.7 48.1 %shard_map.112 = f32[26,32,128]{2,1,0:T(8,128)} custom-call(bf16[26,256,128]{2,1,0:T(8,128)(2,1)} %bitcast.34, s32[26,1,256]{2,1,0:T(1,128)} %broadcast_in_dim.18.keys), custom_call_target="tpu_custom_call" | custom-call | tf_op jit(solution)/shard_map/pallas_call | solution.py:216
  62.8 1.2 %multiply_reduce_fusion = f32[26,32]{1,0:T(8,128)S(1)} fusion(f32[26,32,128]{2,1,0:T(8,128)} %shard_map.112), kind=kLoop, calls=%fused_computation.7 | loop fusion | flops 212160 | bytes 429312 | tf_op jit(solution)/shard_map/reduce_sum | solution.py:273
  64.0 0.0 copy-done.8
  64.0 0.6 sqrt_add_fusion
  64.6 0.0 copy-done.4
  64.6 1.9 %divide_subtract_fusion = f32[26,32,128]{2,1,0:T(8,128)} fusion(f32[26,32,128]{2,1,0:T(8,128)S(1)} %copy-done.4, f32[26,32,128]{2,1,0:T(8,128)} %shard_map.112, f32[26,32]{1,0:T(8,128)S(1)} %get-tuple-element.9), kind=kLoop, calls=%fused_computation.6 | loop fusion | flops 319488 | bytes 1281280 | tf_op jit(solution)/shard_map/sub | solution.py:274
  66.6 1.3 %slice.20 = f32[256,1,128]{2,1,0:T(1,128)S(1)} slice(f32[256,27,128]{2,1,0:T(8,128)} %copy-done.1), slice={[0:256], [0:1], [0:128]} | slice | bytes 262144 | tf_op jit(solution)/shard_map/slice | solution.py:270
  67.9 0.1 copy.24
  68.0 0.9 %fusion.6 = bf16[256,128]{0,1:T(8,128)(2,1)S(1)} fusion(f32[256,479]{0,1:T(8,128)} %copy-done.2, f32[256,1,128]{0,2,1:T(8,128)S(1)} %copy.24), kind=kLoop, calls=%fused_computation.11 | loop fusion | flops 65536 | bytes 327680 | tf_op jit(solution)/shard_map/convert_element_type | solution.py:270
  68.9 0.7 %copy.22 = bf16[256,128]{1,0:T(8,128)(2,1)} copy(bf16[256,128]{0,1:T(8,128)(2,1)S(1)} %fusion.6) | data formatting | bytes 131072
  (1 shorter events, 0.0 us)
Async XLA Ops:
  0.6 1.2 %copy-start = (bf16[479,1024]{1,0:T(8,128)(2,1)S(1)}, bf16[479,1024]{1,0:T(8,128)(2,1)}, u32[]{:S(2)}) copy-start(bf16[479,1024]{1,0:T(8,128)(2,1)} %param.12) | copy-start | bytes 2942980
  0.6 3.5 %copy-start.3 = (bf16[351,729]{1,0:T(8,128)(2,1)S(1)}, bf16[351,729]{1,0:T(8,128)(2,1)}, u32[]{:S(2)}) copy-start(bf16[351,729]{1,0:T(8,128)(2,1)} %constant.76) | copy-start | bytes 1535278
  3.3 0.8 %copy-start.2 = (f32[256,479]{0,1:T(8,128)}, f32[256,479]{0,1:T(8,128)S(1)}, u32[]{:S(2)}) copy-start(f32[256,479]{0,1:T(8,128)S(1)} %fusion.29) | copy-start | bytes 1471492
  7.9 2.7 %copy-start.5 = (bf16[256,128]{1,0:T(8,128)(2,1)S(1)}, bf16[256,128]{1,0:T(8,128)(2,1)}, u32[]{:S(2)}) copy-start(bf16[256,128]{1,0:T(8,128)(2,1)} %param.10) | copy-start | bytes 196612
  11.4 2.5 %copy-start.1 = (f32[256,27,128]{2,1,0:T(8,128)}, f32[256,27,128]{2,1,0:T(8,128)S(1)}, u32[]{:S(2)}) copy-start(f32[256,27,128]{2,1,0:T(8,128)S(1)} %fusion) | copy-start | bytes 10616836
  12.0 2.0 %copy-start.6 = (s32[256,26]{0,1:T(8,128)S(1)}, s32[256,26]{0,1:T(8,128)}, u32[]{:S(2)}) copy-start(s32[256,26]{0,1:T(8,128)} %param.14) | copy-start | bytes 79876
  12.0 2.0 %copy-start.7 = (s32[256,26,1]{0,2,1:T(1,128)S(1)}, s32[256,26,1]{0,2,1:T(1,128)}, u32[]{:S(2)}) copy-start(s32[256,26,1]{0,2,1:T(1,128)} %param.13) | copy-start | bytes 79876
  14.0 50.0 %copy-start.8 = (f32[26,32]{1,0:T(8,128)S(1)}, f32[26,32]{1,0:T(8,128)}, u32[]{:S(2)}) copy-start(f32[26,32]{1,0:T(8,128)} %param.16) | copy-start | bytes 9988
  14.0 50.7 %copy-start.4 = (f32[26,32,128]{2,1,0:T(8,128)S(1)}, f32[26,32,128]{2,1,0:T(8,128)}, u32[]{:S(2)}) copy-start(f32[26,32,128]{2,1,0:T(8,128)} %param.15) | copy-start | bytes 1277956
